TPU v7x, 16 devices: a whole 2x2x2 slice. The times are simulated.
16 devices in a mesh: rep: 1, dp: 16 (over x, y, z, core).
Axes of the slice: x: 2, y: 2, z: 2, core: 2. Of those that a mesh axis runs over, the one named last changes fastest.
Arguments:
- x: bfloat16 [16, 2048, 1280], P(('rep', 'dp'))
- dy: bfloat16 [16, 2048, 1280], P(('rep', 'dp'))
- w_gate: bfloat16 [2, 1280, 5120], P(None, 'dp')
- w_up: bfloat16 [2, 1280, 5120], P(None, 'dp')
- w_down: bfloat16 [2, 5120, 1280], P(None, 'dp')
- m_w_gate: float32 [2, 1280, 5120], P(None, 'dp')
- m_w_up: float32 [2, 1280, 5120], P(None, 'dp')
- m_w_down: float32 [2, 5120, 1280], P(None, 'dp')
- v_w_gate: float32 [2, 1280, 5120], P(None, 'dp')
- v_w_up: float32 [2, 1280, 5120], P(None, 'dp')
- v_w_down: float32 [2, 5120, 1280], P(None, 'dp')
Outputs:
- output 1: bfloat16 [2, 1280, 5120], P('rep', 'dp')
- output 2: bfloat16 [2, 1280, 5120], P('rep', 'dp')
- output 3: bfloat16 [2, 5120, 1280], P('rep', 'dp')
- output 4: float32 [2, 1280, 5120], P('rep', 'dp')
- output 5: float32 [2, 1280, 5120], P('rep', 'dp')
- output 6: float32 [2, 5120, 1280], P('rep', 'dp')
- output 7: float32 [2, 1280, 5120], P('rep', 'dp')
- output 8: float32 [2, 1280, 5120], P('rep', 'dp')
- output 9: float32 [2, 5120, 1280], P('rep', 'dp')
All inputs are finite; a program needn't handle non-finite values.
Results may differ from a plain program's by a relative error of at most 0.0224.
Values are sent between devices in bfloat16 or wider.
A program may use at most 2 GiB of HBM per device.

v0:
```python
import jax
import jax.numpy as jnp
from jax import lax
from jax.sharding import PartitionSpec as P

NAMES = ("w_gate", "w_up", "w_down")


def matmul(a, w):
    return jnp.dot(a, w, preferred_element_type=jnp.float32).astype(jnp.bfloat16)


def normed(h):
    wide = h.astype(jnp.float32)
    scale = lax.rsqrt(jnp.mean(wide**2, -1, keepdims=True) + 1e-6)
    return (wide * scale).astype(jnp.bfloat16)


def layer(h, w):
    a = normed(h)
    gate = jnp.dot(a, w["w_gate"], preferred_element_type=jnp.float32)
    up = jnp.dot(a, w["w_up"], preferred_element_type=jnp.float32)
    return h + matmul((jax.nn.silu(gate) * up).astype(jnp.bfloat16), w["w_down"])


def adamw(w, m, v, g):
    m = 0.9 * m + 0.1 * g
    v = 0.95 * v + 0.05 * g * g
    step = m * lax.rsqrt(v + 1e-8) + 0.1 * w
    return (w - 0.02 * step).astype(jnp.bfloat16), m, v


def clipped(gradients, sum_of_squares, count):
    factor = jnp.minimum(1.0, 0.5 * lax.rsqrt(sum_of_squares / count + 1e-30))
    return [g * factor for g in gradients]


def solution(mesh):
    def fetched(weights, number):
        return {name: lax.all_gather(w[number], "dp", axis=0, tiled=True) for name, w in zip(NAMES, weights, strict=True)}

    def step(x, dy, *arrays):
        weights, m, v = (arrays[i : i + 3] for i in (0, 3, 6))
        layers = weights[0].shape[0]
        h, kept = x[0], []
        for number in range(layers):
            kept.append(h)
            h = layer(h, fetched(weights, number))
        by_h, mine = dy[0], [None] * layers
        for number in reversed(range(layers)):
            _, back = jax.vjp(lambda w, h: layer(h, w), fetched(weights, number), kept[number])
            by_w, by_h = back(by_h)
            mine[number] = [lax.psum_scatter(by_w[name], "dp", scatter_dimension=0, tiled=True) for name in NAMES]
        gradients = [jnp.stack([mine[number][i] for number in range(layers)]).astype(jnp.float32) for i in range(3)]
        squares = lax.psum(sum(jnp.sum(g * g) for g in gradients), "dp")
        gradients = clipped(gradients, squares, lax.psum(1, "dp") * sum(g.size for g in gradients))
        new = [adamw(w.astype(jnp.float32), m, v, g) for w, m, v, g in zip(weights, m, v, gradients, strict=True)]
        return tuple(one[which] for which in range(3) for one in new)

    states, cut = P(("rep", "dp"), None, None), P(None, "dp", None)
    return jax.shard_map(
        step,
        mesh=mesh,
        in_specs=(states, states) + (cut,) * 9,
        out_specs=(P("rep", "dp", None),) * 9,
        check_vma=False,
    )
```

profile of v0, /device:TPU:0, one launch (start us, length us, event | category | flops | bytes accessed | tf_op | source)
XLA Modules:
  0.0 1506.4 jit_solution(9353832291891131249)
XLA Ops:
  7.2 0.0 all-gather.13.cloned.1.call-start
  7.2 2.7 fusion.105
  9.9 0.0 all-gather.13.cloned.1.call-update
  9.9 0.0 all-gather.15.cloned.1.call-start
  10.0 2.7 fusion.104
  12.6 0.0 all-gather.15.cloned.1.call-update
  12.6 0.0 all-gather.17.cloned.1.call-start
  12.7 2.7 fusion.103
  15.4 0.0 all-gather.17.cloned.1.call-update
  15.4 0.0 all-gather.21.cloned.1.call-start
  15.4 0.5 all-gather.21.cloned.1.call-update
  16.0 0.0 all-gather.23.cloned.1.call-start
  16.0 0.5 all-gather.23.cloned.1.call-update
  16.5 0.0 all-gather.19.cloned.1.call-start
  16.6 0.5 all-gather.19.cloned.1.call-update
  17.1 0.0 reduce-scatter.15.cloned.1.call-start
  17.2 7.9 copy.20
  25.1 3.6 fusion.36
  28.7 7.9 copy.21
  36.6 41.1 %all-gather.13.cloned.1.call-done = bf16[1,1280,5120]{2,1,0:T(8,128)(2,1)} async-done(((bf16[1,80,5120]{2,1,0:T(8,128)(2,1)}), bf16[1,1280,5120]{2,1,0:T(8,128)(2,1)}) %all-gather.13.cloned.1.call-update) | async-done | bytes 13107216 | tf_op jit(solution)/shard_map/all_gather | solution.py:40
  77.7 35.0 %fusion.34 = f32[2048,5120]{1,0:T(8,128)} fusion(bf16[1,1280,5120]{2,1,0:T(8,128)(2,1)} %all-gather.13.cloned.1.call-done, bf16[1,2048,1280]{1,2,0:T(8,128)(2,1)} %copy.20, f32[2048]{0:T(1024)S(1)} %add_rsqrt_fusion), kind=kOutput, calls=%fused_computation.49 | convolution fusion | flops 26851409920 | bytes 60301312 | tf_op jit(solution)/shard_map/dot_general | solution.py:21
  112.7 31.9 %all-gather.15.cloned.1.call-done = bf16[1,1280,5120]{2,1,0:T(8,128)(2,1)} async-done(((bf16[1,80,5120]{2,1,0:T(8,128)(2,1)}), bf16[1,1280,5120]{2,1,0:T(8,128)(2,1)}) %all-gather.15.cloned.1.call-update) | async-done | bytes 13107216 | tf_op jit(solution)/shard_map/all_gather | solution.py:40
  144.6 51.6 %multiply_convert_fusion.1 = (bf16[2048,5120]{1,0:T(8,128)(2,1)}, f32[2048,5120]{1,0:T(8,128)}) fusion(f32[2048,5120]{1,0:T(8,128)} %fusion.34, bf16[1,1280,5120]{2,1,0:T(8,128)(2,1)} %all-gather.15.cloned.1.call-done, bf16[1,2048,1280]{1,2,0:T(8,128)(2,1)} %copy.20, f32[2048]{0:T(1024)S(1)} %add_rsqrt_fusion), kind=kOutput, calls=%fused_computation.17 | convolution fusion | flops 26914324480 | bytes 123215872 | tf_op jit(solution)/shard_map/dot_general | solution.py:22
  196.2 15.2 %all-gather.17.cloned.1.call-done = bf16[1,5120,1280]{2,1,0:T(8,128)(2,1)} async-done(((bf16[1,320,1280]{2,1,0:T(8,128)(2,1)}), bf16[1,5120,1280]{2,1,0:T(8,128)(2,1)}) %all-gather.17.cloned.1.call-update) | async-done | bytes 13107216 | tf_op jit(solution)/shard_map/all_gather | solution.py:40
  211.4 48.6 %fusion.40 = (f32[2048]{0:T(1024)S(1)}, bf16[2048,1280]{0,1:T(8,128)(2,1)}) fusion(bf16[2048,5120]{1,0:T(8,128)(2,1)} %get-tuple-element.24, bf16[1,5120,1280]{2,1,0:T(8,128)(2,1)} %all-gather.17.cloned.1.call-done, bf16[1,2048,1280]{1,2,0:T(8,128)(2,1)} %copy.20), kind=kOutput, calls=%fused_computation.58 | convolution fusion | flops 26856650752 | bytes 44572672 | tf_op jit(solution)/shard_map/dot_general | solution.py:10
  260.0 18.2 %all-gather.21.cloned.1.call-done = bf16[1,5120,1280]{2,1,0:T(8,128)(2,1)} async-done(((bf16[1,320,1280]{2,1,0:T(8,128)(2,1)}), bf16[1,5120,1280]{2,1,0:T(8,128)(2,1)}) %all-gather.21.cloned.1.call-update) | async-done | bytes 13107216 | tf_op jit(solution)/shard_map/all_gather | solution.py:40
  278.2 34.2 %convolution_convert_fusion.1 = bf16[2048,5120]{1,0:T(8,128)(2,1)} fusion(bf16[1,5120,1280]{2,1,0:T(8,128)(2,1)} %all-gather.21.cloned.1.call-done, bf16[1,2048,1280]{2,1,0:T(8,128)(2,1)} %param.12), kind=kOutput, calls=%fused_computation.29 | convolution fusion | flops 26854031360 | bytes 39321600 | tf_op jit(solution)/shard_map/transpose(jvp())/dot_general | solution.py:10
  312.4 32.5 %all-gather.23.cloned.1.call-done = bf16[1,1280,5120]{2,1,0:T(8,128)(2,1)} async-done(((bf16[1,80,5120]{2,1,0:T(8,128)(2,1)}), bf16[1,1280,5120]{2,1,0:T(8,128)(2,1)}) %all-gather.23.cloned.1.call-update) | async-done | bytes 13107216 | tf_op jit(solution)/shard_map/all_gather | solution.py:40
  344.9 35.1 %fusion.21 = f32[2048,5120]{1,0:T(8,128)} fusion(bf16[1,1280,5120]{2,1,0:T(8,128)(2,1)} %all-gather.23.cloned.1.call-done, bf16[2048,1280]{0,1:T(8,128)(2,1)} %get-tuple-element.27, f32[2048]{0:T(1024)S(1)} %fusion.91), kind=kOutput, calls=%fused_computation.36 | convolution fusion | flops 26851409920 | bytes 60301312 | tf_op jit(solution)/shard_map/jvp()/dot_general | solution.py:22
  380.0 31.6 %all-gather.19.cloned.1.call-done = bf16[1,1280,5120]{2,1,0:T(8,128)(2,1)} async-done(((bf16[1,80,5120]{2,1,0:T(8,128)(2,1)}), bf16[1,1280,5120]{2,1,0:T(8,128)(2,1)}) %all-gather.19.cloned.1.call-update) | async-done | bytes 13107216 | tf_op jit(solution)/shard_map/all_gather | solution.py:40
  411.6 59.6 %fusion.2 = (bf16[2048,5120]{1,0:T(8,128)(2,1)}, f32[2048,5120]{1,0:T(8,128)}) fusion(f32[2048,5120]{1,0:T(8,128)} %fusion.21, bf16[2048,5120]{1,0:T(8,128)(2,1)} %convolution_convert_fusion.1, bf16[1,1280,5120]{2,1,0:T(8,128)(2,1)} %all-gather.19.cloned.1.call-done, bf16[2048,1280]{0,1:T(8,128)(2,1)} %get-tuple-element.27, f32[2048]{0:T(1024)S(1)} %fusion.91), kind=kOutput, calls=%fused_computation.8 | convolution fusion | flops 26977239040 | bytes 144187392 | tf_op jit(solution)/shard_map/jvp()/dot_general | solution.py:21
  471.2 35.7 %fusion.46 = bf16[2048,1280]{0,1:T(8,128)(2,1)} fusion(bf16[2048,5120]{1,0:T(8,128)(2,1)} %get-tuple-element.28, bf16[1,1280,5120]{2,1,0:T(8,128)(2,1)} %all-gather.19.cloned.1.call-done), kind=kOutput, calls=%fused_computation.62 | convolution fusion | flops 26843545600 | bytes 39321600 | tf_op jit(solution)/shard_map/transpose(jvp())/dot_general | solution.py:21
  506.9 41.0 %fusion.42 = (f32[2048]{0:T(1024)S(1)}, bf16[2048,1280]{0,1:T(8,128)(2,1)}) fusion(bf16[2048,1280]{0,1:T(8,128)(2,1)S(1)} %copy-done.3, bf16[2048,1280]{0,1:T(8,128)(2,1)} %fusion.46, bf16[1,1280,5120]{2,1,0:T(8,128)(2,1)} %all-gather.23.cloned.1.call-done, bf16[2048,5120]{1,0:T(8,128)(2,1)} %convolution_convert_fusion.1, f32[2048,5120]{1,0:T(8,128)} %get-tuple-element.29), kind=kOutput, calls=%fused_computation.60 | convolution fusion | flops 26922186752 | bytes 91758592 | tf_op jit(solution)/shard_map/transpose(jvp())/dot_general | solution.py:22
  548.0 12.3 fusion.59
  560.3 33.8 %convolution_convert_fusion.2 = bf16[5120,1280]{1,0:T(8,128)(2,1)} fusion(bf16[2048,5120]{1,0:T(8,128)(2,1)} %get-tuple-element.24, bf16[2048,1280]{0,1:T(8,128)(2,1)} %fusion.59), kind=kOutput, calls=%fused_computation.30 | convolution fusion | flops 26850099200 | bytes 39321600 | tf_op jit(solution)/shard_map/transpose(jvp())/dot_general | solution.py:10
  594.1 0.0 reduce-scatter.15.cloned.1.call-update
  594.1 0.0 reduce-scatter.17.cloned.1.call-start
  594.1 42.0 %fusion.15 = bf16[5120,1280]{1,0:T(8,128)(2,1)} fusion(f32[2048,5120]{1,0:T(8,128)} %fusion.21, bf16[1,2048,1280]{2,1,0:T(8,128)(2,1)} %param.12, f32[2048,5120]{1,0:T(8,128)} %get-tuple-element.29), kind=kOutput, calls=%fused_computation.24 | convolution fusion | flops 26913013760 | bytes 102236160 | tf_op jit(solution)/shard_map/transpose(jvp())/dot_general | solution.py:10
  636.1 0.0 reduce-scatter.17.cloned.1.call-update
  636.2 0.0 reduce-scatter.11.cloned.1.call-start
  636.2 35.1 %convolution_convert_fusion = bf16[2048,5120]{1,0:T(8,128)(2,1)} fusion(bf16[2048,1280]{0,1:T(8,128)(2,1)} %fusion.59, bf16[1,5120,1280]{2,1,0:T(8,128)(2,1)} %all-gather.17.cloned.1.call-done), kind=kOutput, calls=%fused_computation.28 | convolution fusion | flops 26854031360 | bytes 39321600 | tf_op jit(solution)/shard_map/transpose(jvp())/dot_general | solution.py:10
  671.3 38.0 %fusion.20 = bf16[1280,5120]{1,0:T(8,128)(2,1)} fusion(bf16[2048,5120]{1,0:T(8,128)(2,1)} %convolution_convert_fusion, f32[2048,5120]{1,0:T(8,128)} %fusion.34, bf16[1,2048,1280]{1,2,0:T(8,128)(2,1)} %copy.20, f32[2048]{0:T(1024)S(1)} %copy-done.17), kind=kOutput, calls=%fused_computation.27 | convolution fusion | flops 26920878080 | bytes 81272832 | tf_op jit(solution)/shard_map/transpose(jvp())/dot_general | solution.py:22
  709.3 0.0 reduce-scatter.13.cloned.1.call-start
  709.3 0.6 copy-done.13
  709.9 38.1 %fusion.16 = bf16[1280,5120]{1,0:T(8,128)(2,1)} fusion(bf16[2048,5120]{1,0:T(8,128)(2,1)} %convolution_convert_fusion.1, bf16[2048,1280]{0,1:T(8,128)(2,1)} %get-tuple-element.27, f32[2048]{0:T(1024)S(1)} %copy-done.13, f32[2048,5120]{1,0:T(8,128)} %get-tuple-element.29), kind=kOutput, calls=%fused_computation.25 | convolution fusion | flops 26920878080 | bytes 81272832 | tf_op jit(solution)/shard_map/transpose(jvp())/dot_general | solution.py:22
  748.0 0.0 reduce-scatter.7.cloned.1.call-start
  748.1 48.1 %fusion.17 = bf16[1280,5120]{1,0:T(8,128)(2,1)} fusion(f32[2048,5120]{1,0:T(8,128)} %fusion.34, f32[2048,5120]{1,0:T(8,128)} %get-tuple-element.25, bf16[2048,5120]{1,0:T(8,128)(2,1)} %convolution_convert_fusion, bf16[1,2048,1280]{1,2,0:T(8,128)(2,1)} %copy.20, f32[2048]{0:T(1024)S(1)} %copy-done.17), kind=kOutput, calls=%fused_computation.26 | convolution fusion | flops 26973306880 | bytes 123215872 | tf_op jit(solution)/shard_map/transpose(jvp())/dot_general | solution.py:21
  796.2 0.0 reduce-scatter.9.cloned.1.call-start
  796.3 33.8 %convolution_convert_fusion.3 = bf16[1280,5120]{1,0:T(8,128)(2,1)} fusion(bf16[2048,5120]{1,0:T(8,128)(2,1)} %get-tuple-element.28, bf16[2048,1280]{0,1:T(8,128)(2,1)} %get-tuple-element.27, f32[2048]{0:T(1024)S(1)} %copy-done.13), kind=kOutput, calls=%fused_computation.31 | convolution fusion | flops 26851409920 | bytes 39329792 | tf_op jit(solution)/shard_map/transpose(jvp())/dot_general | solution.py:21
  830.1 0.0 reduce-scatter.15.cloned.1.call-done
  830.1 41.4 %reduce-scatter.17.cloned.1.call-done = bf16[320,1280]{1,0:T(8,128)(2,1)} async-done(((bf16[5120,1280]{1,0:T(8,128)(2,1)}), bf16[320,1280]{1,0:T(8,128)(2,1)}) %reduce-scatter.17.cloned.1.call-update) | async-done | bytes 819216 | tf_op jit(solution)/shard_map/reduce_scatter | solution.py:53
  871.5 2.8 fusion.81
  874.4 139.0 %reduce-scatter.11.cloned.1.call-done = bf16[80,5120]{1,0:T(8,128)(2,1)} async-done(((bf16[1280,5120]{1,0:T(8,128)(2,1)}), bf16[80,5120]{1,0:T(8,128)(2,1)}) %reduce-scatter.11.cloned.1.call-update) | async-done | bytes 819216 | tf_op jit(solution)/shard_map/reduce_scatter | solution.py:53
  1013.4 141.7 %reduce-scatter.13.cloned.1.call-done = bf16[80,5120]{1,0:T(8,128)(2,1)} async-done(((bf16[1280,5120]{1,0:T(8,128)(2,1)}), bf16[80,5120]{1,0:T(8,128)(2,1)}) %reduce-scatter.13.cloned.1.call-update) | async-done | bytes 819216 | tf_op jit(solution)/shard_map/reduce_scatter | solution.py:53
  1155.0 3.0 fusion.80
  1158.0 138.8 %reduce-scatter.7.cloned.1.call-done = bf16[80,5120]{1,0:T(8,128)(2,1)} async-done(((bf16[1280,5120]{1,0:T(8,128)(2,1)}), bf16[80,5120]{1,0:T(8,128)(2,1)}) %reduce-scatter.7.cloned.1.call-update) | async-done | bytes 819216 | tf_op jit(solution)/shard_map/reduce_scatter | solution.py:53
  1296.8 141.7 %reduce-scatter.9.cloned.1.call-done = bf16[80,5120]{1,0:T(8,128)(2,1)} async-done(((bf16[1280,5120]{1,0:T(8,128)(2,1)}), bf16[80,5120]{1,0:T(8,128)(2,1)}) %reduce-scatter.9.cloned.1.call-update) | async-done | bytes 819216 | tf_op jit(solution)/shard_map/reduce_scatter | solution.py:53
  1438.5 2.8 fusion.79
  1443.3 35.4 %psum.7 = f32[]{:T(128)} all-reduce(f32[]{:T(128)S(6)} %add.99), channel_id=1, replica_groups=mesh['rep'=1,'dp'=16] {'dp'}, use_global_device_ids=true, to_apply=%region_12.13 | all-reduce | flops 1 | bytes 8 | tf_op jit(solution)/shard_map/psum | solution.py:55
  1479.5 7.4 fusion.87
  1486.9 1.2 copy-done.8
  1488.1 0.9 copy-done.9
  1489.0 0.9 copy-done.10
  1490.0 9.1 fusion.78
  (39 shorter events, 0.2 us)
Async XLA Ops:
  7.2 70.5 %all-gather.13.cloned.1.call-start = ((), (), s32[]{:S(2)}) async-start(), calls=%async_computation.12 | async-start | bytes 13926400 | tf_op jit(solution)/shard_map/all_gather | solution.py:40
  9.9 134.7 %all-gather.15.cloned.1.call-start = ((), (), s32[]{:S(2)}) async-start(), calls=%async_computation.13 | async-start | bytes 13926400 | tf_op jit(solution)/shard_map/all_gather | solution.py:40
  12.6 198.8 %all-gather.17.cloned.1.call-start = ((), (), s32[]{:S(2)}) async-start(), calls=%async_computation.14 | async-start | bytes 13926400 | tf_op jit(solution)/shard_map/all_gather | solution.py:40
  15.4 262.8 %all-gather.21.cloned.1.call-start = ((), (), s32[]{:S(2)}) async-start(), calls=%async_computation.16 | async-start | bytes 13926400 | tf_op jit(solution)/shard_map/all_gather | solution.py:40
  16.0 328.9 %all-gather.23.cloned.1.call-start = ((), (), s32[]{:S(2)}) async-start(), calls=%async_computation.17 | async-start | bytes 13926400 | tf_op jit(solution)/shard_map/all_gather | solution.py:40
  16.5 395.1 %all-gather.19.cloned.1.call-start = ((), (), s32[]{:S(2)}) async-start(), calls=%async_computation.15 | async-start | bytes 13926400 | tf_op jit(solution)/shard_map/all_gather | solution.py:40
  17.1 813.0 %reduce-scatter.15.cloned.1.call-start = ((), (), s32[]{:S(2)}) async-start(), calls=%async_computation.10 | async-start | bytes 13926400 | tf_op jit(solution)/shard_map/reduce_scatter | solution.py:53
  28.7 115.9 %copy-start.16 = (f32[2048]{0:T(1024)}, f32[2048]{0:T(1024)S(1)}, u32[]{:S(2)}) copy-start(f32[2048]{0:T(1024)S(1)} %add_rsqrt_fusion) | copy-start | bytes 24580
  260.0 52.4 %copy-start.14 = (f32[2048]{0:T(1024)}, f32[2048]{0:T(1024)S(1)}, u32[]{:S(2)}) copy-start(f32[2048]{0:T(1024)S(1)} %get-tuple-element.26) | copy-start | bytes 24580
  260.0 151.6 %copy-start.11 = (f32[2048]{0:T(1024)}, f32[2048]{0:T(1024)S(1)}, u32[]{:S(2)}) copy-start(f32[2048]{0:T(1024)S(1)} %fusion.91) | copy-start | bytes 24580
  471.2 35.7 %copy-start.3 = (bf16[2048,1280]{0,1:T(8,128)(2,1)S(1)}, bf16[2048,1280]{0,1:T(8,128)(2,1)}, u32[]{:S(2)}) copy-start(bf16[2048,1280]{0,1:T(8,128)(2,1)} %get-tuple-element.27) | copy-start | bytes 15728644
  506.9 41.0 %copy-start.15 = (f32[2048]{0:T(1024)S(1)}, f32[2048]{0:T(1024)}, u32[]{:S(2)}) copy-start(f32[2048]{0:T(1024)} %copy-done.14) | copy-start | bytes 24580
  506.9 41.0 %copy-start.12 = (f32[2048]{0:T(1024)S(1)}, f32[2048]{0:T(1024)}, u32[]{:S(2)}) copy-start(f32[2048]{0:T(1024)} %copy-done.11) | copy-start | bytes 24580
  594.1 277.4 %reduce-scatter.17.cloned.1.call-start = ((), (), s32[]{:S(2)}) async-start(), calls=%async_computation.11 | async-start | bytes 13926400 | tf_op jit(solution)/shard_map/reduce_scatter | solution.py:53
  636.1 35.1 %copy-start.17 = (f32[2048]{0:T(1024)S(1)}, f32[2048]{0:T(1024)}, u32[]{:S(2)}) copy-start(f32[2048]{0:T(1024)} %copy-done.16) | copy-start | bytes 24580
  636.2 377.2 %reduce-scatter.11.cloned.1.call-start = ((), (), s32[]{:S(2)}) async-start(), calls=%async_computation.8 | async-start | bytes 13926400 | tf_op jit(solution)/shard_map/reduce_scatter | solution.py:53
  709.2 0.7 copy-start.13
  709.3 445.8 %reduce-scatter.13.cloned.1.call-start = ((), (), s32[]{:S(2)}) async-start(), calls=%async_computation.9 | async-start | bytes 13926400 | tf_op jit(solution)/shard_map/reduce_scatter | solution.py:53
  748.0 548.8 %reduce-scatter.7.cloned.1.call-start = ((), (), s32[]{:S(2)}) async-start(), calls=%async_computation.6 | async-start | bytes 13926400 | tf_op jit(solution)/shard_map/reduce_scatter | solution.py:53
  796.2 642.3 %reduce-scatter.9.cloned.1.call-start = ((), (), s32[]{:S(2)}) async-start(), calls=%async_computation.7 | async-start | bytes 13926400 | tf_op jit(solution)/shard_map/reduce_scatter | solution.py:53
  830.1 649.3 %copy-start = (bf16[2,320,1280]{2,1,0:T(8,128)(2,1)S(1)}, bf16[2,320,1280]{2,1,0:T(8,128)(2,1)}, u32[]{:S(2)}) copy-start(bf16[2,320,1280]{2,1,0:T(8,128)(2,1)} %param.15) | copy-start | bytes 4915204
  1155.0 331.8 %copy-start.1 = (bf16[2,80,5120]{2,1,0:T(8,128)(2,1)S(1)}, bf16[2,80,5120]{2,1,0:T(8,128)(2,1)}, u32[]{:S(2)}) copy-start(bf16[2,80,5120]{2,1,0:T(8,128)(2,1)} %param.13) | copy-start | bytes 4915204
  1479.4 7.5 copy-start.2
  1479.4 7.5 copy-start.4
  1479.4 7.5 copy-start.5
  1479.4 7.5 copy-start.6
  1479.4 7.5 copy-start.7
  1479.4 8.7 copy-start.8
  1479.4 9.6 copy-start.9
  1479.4 10.5 copy-start.10
Sparse Core Ops, SparseCore 0:
  10.8 66.8 all-gather.12
  80.5 64.0 all-gather.14
  147.4 64.0 all-gather.16
  214.1 64.0 all-gather.20
  280.8 64.0 all-gather.22
  347.6 64.0 all-gather.18
  594.2 135.4 reduce-scatter.14
  732.0 139.4 reduce-scatter.16
  873.8 139.4 reduce-scatter.10
  1015.5 139.4 reduce-scatter.12
  1157.3 139.4 reduce-scatter.6
  1299.0 139.4 reduce-scatter.8
where the time goes:
time: 1510 us
  waiting for transfers between devices  775 us (51%)
  matrix products  610 us (40%)
  other arithmetic  41 us (3%)
  blocking collectives  35.4 us (2%)
  local copies, waits for them, and re-layouts  27.6 us (2%)
  between operations  17.6 us (1%)
    reduce_scatter x6, waiting for transfers between devices, step(): lax.psum_scatter(by_w[name], 'dp', scatter_dimension=0, tiled=True)  603 us
    dot_general x5, matrix products, layer(): gate = jnp.dot(a, w['w_gate'], preferred_element_type=jnp.float32)  212 us
    dot_general x5, matrix products, layer(): up = jnp.dot(a, w['w_up'], preferred_element_type=jnp.float32)  204 us
    dot_general x5, matrix products, matmul(): jnp.dot(a, w, preferred_element_type=jnp.float32).astype(jnp.bfloat16)  194 us
    all_gather x6, waiting for transfers between devices, fetched(): lax.all_gather(w[number], 'dp', axis=0, tiled=True)  170 us
    psum x1, blocking collectives, step(): squares = lax.psum(sum((jnp.sum(g * g) for g in gradients)), 'dp')  35.4 us
  transfers between devices with their start and end apart: 12, of which 11 were waited for; matrix products, arithmetic and copies ran while one was open for 31% of the time, Pallas kernels for 0%

commit v1 on v0

v1 whole, which is shorter than its diff:
```python
import jax
import jax.numpy as jnp
from jax import lax
from jax.experimental import pallas as pl
from jax.experimental.pallas import tpu as pltpu
from jax.sharding import PartitionSpec as P

F32, BF16 = jnp.float32, jnp.bfloat16


def normed(h):
    wide = h.astype(F32)
    scale = lax.rsqrt(jnp.mean(wide**2, -1, keepdims=True) + 1e-6)
    return (wide * scale).astype(BF16)


def adamw(w, m, v, g):
    m = 0.9 * m + 0.1 * g
    v = 0.95 * v + 0.05 * g * g
    step = m * lax.rsqrt(v + 1e-8) + 0.1 * w
    return (w - 0.02 * step).astype(BF16), m, v


def dot(a, b, contract):
    return lax.dot_general(a, b, ((contract[:1], contract[1:]), ((), ())), preferred_element_type=F32)


def everywhere(n, part):
    def kernel(part_ref, out_ref, slots, send_sem, recv_sem):
        me = lax.axis_index("dp")
        barrier = pltpu.get_barrier_semaphore()
        for k in range(1, n):
            pl.semaphore_signal(barrier, inc=1, device_id={"dp": lax.rem(me + k, n)}, device_id_type=pl.DeviceIdType.MESH)
        pl.semaphore_wait(barrier, n - 1)
        copies = []
        for k in range(1, n):
            copy = pltpu.make_async_remote_copy(
                src_ref=part_ref,
                dst_ref=slots.at[k],
                send_sem=send_sem.at[k],
                recv_sem=recv_sem.at[k],
                device_id={"dp": lax.rem(me + k, n)},
                device_id_type=pl.DeviceIdType.MESH,
            )
            copy.start()
            copies.append(copy)
        total = part_ref[...]
        for k, copy in enumerate(copies, 1):
            copy.wait()
            total = total + slots[k]
        out_ref[...] = total

    return pl.pallas_call(
        kernel,
        out_shape=jax.ShapeDtypeStruct((8, 128), F32),
        in_specs=[pl.BlockSpec(memory_space=pltpu.VMEM)],
        out_specs=pl.BlockSpec(memory_space=pltpu.VMEM),
        scratch_shapes=[pltpu.VMEM((n, 8, 128), F32), pltpu.SemaphoreType.DMA((n,)), pltpu.SemaphoreType.DMA((n,))],
        compiler_params=pltpu.CompilerParams(collective_id=0, has_side_effects=True),
    )(part)


def across(bits):
    owner = lax.axis_index("dp")
    for bit in (8, 4, 2, 1):
        if bits & bit:
            owner = owner + bit - 2 * bit * (owner // bit % 2)
    return owner


def thirds(cols):
    later = cols // 128 // 3 * 128
    return [(0, cols - 2 * later), (cols - 2 * later, later), (cols - later, later)]


class Gather:
    SENDS = [(0, 8), (0, 4), (0, 2), (8, 4), (4, 2), (2, 8), (12, 2), (6, 8), (10, 4)]
    HANDED = [0, 8, 4, 2, 12, 6, 10, 14]
    COPIES = 17

    def __init__(self, shard, full, send_sem, recv_sem, local_sem):
        rows, cols = shard.shape
        spans = thirds(cols)

        def block(bits, third=None):
            start = pl.multiple_of(across(bits) * rows, 16)
            if third is None:
                return full.at[pl.ds(start, rows), :]
            return full.at[pl.ds(start, rows), pl.ds(spans[third][0], spans[third][1])]

        def copy(k, bits, to, third=None):
            return pltpu.make_async_remote_copy(
                src_ref=shard if bits == 0 else block(bits, third),
                dst_ref=block(bits, third),
                send_sem=send_sem.at[k],
                recv_sem=recv_sem.at[k],
                device_id={"dp": across(to)},
                device_id_type=pl.DeviceIdType.MESH,
            )

        self.far = [copy(k, bits, to, k - 6 if k >= 6 else None) for k, (bits, to) in enumerate(self.SENDS)]
        self.near = [copy(9 + k, bits, 1) for k, bits in enumerate(self.HANDED)]
        self.local = pltpu.make_async_copy(shard, block(0), local_sem)

    def then(self, phase):
        pass

    def before(self, number):
        if number == 0:
            for copy in self.far[:3] + self.near[:1] + [self.local]:
                copy.start()
        elif number < 3:
            for k in range(3 * number - 3, 3 * number):
                self.far[k].wait_recv()
                self.far[k + 3].start()
                self.near[k + 1].start()
        else:
            for k in range(6, 9):
                self.far[k].wait_recv()
            self.near[7].start()

    def last(self):
        for copy in self.near:
            copy.wait_recv()
        for copy in self.far + self.near:
            copy.wait_send()
        self.local.wait()


def meet():
    barrier = pltpu.get_barrier_semaphore()
    for bit in (8, 4, 2, 1):
        pl.semaphore_signal(barrier, inc=1, device_id={"dp": across(bit)}, device_id_type=pl.DeviceIdType.MESH)
    pl.semaphore_wait(barrier, 4)


class Scatter:
    COPIES = 17
    PAIRS = [14, 12, 6, 10, 8, 4, 2, 0]
    LINKS = [[2, 8, 4], [4, 2, 8], [8, 4, 2]]
    SUMS = [[14], [12, 6, 10], [8, 4, 2]]

    @staticmethod
    def scratch(rows, cols):
        one = lambda n, t=BF16: pltpu.VMEM((n, rows, cols), t)
        return [one(8), one(8, F32), one(1), one(3), one(3), one(1), one(3), one(3)] + [
            pltpu.SemaphoreType.DMA((17,)), pltpu.SemaphoreType.DMA((17,)), pltpu.SemaphoreType.DMA((8,))
        ]

    def __init__(self, leave, stay, out, squares, pair, held, *more):
        *buffers, send_sem, recv_sem, local_sem = more
        self.out, self.squares, self.pair, self.held = out, squares, pair, held
        self.going, self.came = buffers[:3], buffers[3:]
        _, self.rows, cols = pair.shape
        self.spans = thirds(cols)

        def copy(k, src, dst, to):
            return pltpu.make_async_remote_copy(
                src_ref=src,
                dst_ref=dst,
                send_sem=send_sem.at[k],
                recv_sem=recv_sem.at[k],
                device_id={"dp": across(to)},
                device_id_type=pl.DeviceIdType.MESH,
            )

        self.near = [copy(k, leave.at[across(m) // 2], pair.at[m // 2], 1) for k, m in enumerate(self.PAIRS)]
        self.loads = [pltpu.make_async_copy(stay.at[across(m) // 2], held.at[m // 2], local_sem.at[k]) for k, m in enumerate(self.PAIRS)]
        self.far = []
        for stage, links in enumerate(self.LINKS):
            made = []
            for i, link in enumerate(links):
                src, dst = self.going[stage].at[i if stage else 0], self.came[stage].at[i if stage else 0]
                if stage == 0:
                    columns = pl.ds(self.spans[i][0], self.spans[i][1])
                    src, dst = src.at[:, columns], dst.at[:, columns]
                made.append(copy(8 + 3 * stage + i, src, dst, link))
            self.far.append(made)

    def ready(self, m):
        k = self.PAIRS.index(m)
        self.near[k].wait_recv()
        self.loads[k].wait()

    def before(self, phase):
        if phase == 0:
            for one in self.near + self.loads:
                one.start()
            return
        stage = phase - 1
        for m in self.SUMS[stage]:
            self.ready(m)
        if stage:
            for copy in self.far[stage - 1]:
                copy.wait_recv()
        for i, m in enumerate(self.SUMS[stage]):

            def add(r, _, i=i, m=m):
                some = pl.ds(pl.multiple_of(r * 16, 16), 16)
                for t, (start, size) in enumerate(self.spans):
                    columns = pl.ds(start, size)
                    value = self.held[m // 2, some, columns] + self.pair[m // 2, some, columns].astype(F32)
                    if stage == 1 and t == i:
                        value = value + self.came[0][0, some, columns].astype(F32)
                    if stage == 2:
                        value = value + self.came[1][i, some, columns].astype(F32)
                    self.going[stage][i, some, columns] = value.astype(BF16)
                return 0

            lax.fori_loop(0, self.rows // 16, add, 0)

    def then(self, phase):
        if phase:
            for copy in self.far[phase - 1]:
                copy.start()

    def last(self):
        self.ready(0)
        for copy in self.far[2]:
            copy.wait_recv()

        def add(r, total):
            some = pl.ds(pl.multiple_of(r * 16, 16), 16)
            value = self.held[0, some, :] + self.pair[0, some, :].astype(F32)
            for i in range(3):
                value = value + self.came[2][i, some, :].astype(F32)
            value = value.astype(BF16)
            self.out[some, :] = value
            value = value.astype(F32)
            value = value * value
            return sum((value[:, at : at + 128] for at in range(0, value.shape[1], 128)), total)

        total = lax.fori_loop(0, self.rows // 16, add, jnp.zeros((16, 128), F32))
        self.squares[...] = total[:8] + total[8:]
        for copy in self.near + self.far[0] + self.far[1] + self.far[2]:
            copy.wait_send()


def hosting(body, steps, operands, in_specs, out_shape, out_specs, tasks, identity, flops, moved, own_scratch=()):
    given, made = len(operands), len(out_shape)
    anywhere = pl.BlockSpec(memory_space=pl.ANY)
    task_ins, task_outs, task_out_specs, scratch, shape_of = [], [], [], [], []
    for arrays, *_ in tasks:
        if len(arrays) == 1:
            _, rows, cols = arrays[0].shape
            task_outs.append([jax.ShapeDtypeStruct((16 * rows, cols), BF16)])
            task_out_specs.append(anywhere)
            more = [pltpu.SemaphoreType.DMA((Gather.COPIES,)), pltpu.SemaphoreType.DMA((Gather.COPIES,)), pltpu.SemaphoreType.DMA(())]
        else:
            _, rows, cols = arrays[0].shape
            task_outs.append([jax.ShapeDtypeStruct((rows, cols), BF16), jax.ShapeDtypeStruct((8, 128), F32)])
            task_out_specs += [pl.BlockSpec((rows, cols), lambda i: (0, 0)), pl.BlockSpec((8, 128), lambda i: (0, 0))]
            more = Scatter.scratch(rows, cols)
        shape_of.append((len(arrays), len(more)))
        task_ins += arrays
        scratch += more
    scratch += list(own_scratch)

    def kernel(*refs):
        refs = list(refs)
        take = lambda k: [refs.pop(0) for _ in range(k)]
        ins = take(given)
        task_in = [take(n) for n, _ in shape_of]
        outs = take(made)
        task_out = [take(len(one)) for one in task_outs]
        running = []
        for (n, k), mine, out, (_, _, *layer) in zip(shape_of, task_in, task_out, tasks, strict=True):
            if n == 1:
                mine = [mine[0].at[layer[0]]]
            running.append((Gather if n == 1 else Scatter)(*mine, *out, *take(k)))
        step = pl.program_id(0)

        def due(now, action):
            wait = 1 if body is None and action == "then" else 0
            todo = sorted((phase, i) for i, (_, when, *_) in enumerate(tasks) for phase in range(4) if when[phase] + wait == now)
            if todo:

                @pl.when(step == now)
                def _():
                    if now == 0 and action == "before":
                        meet()
                    for phase, i in todo:
                        getattr(running[i], action)(phase)

        for now in range(steps):
            due(now, "before")
        if body is not None:
            body(*ins, *outs, *refs)
        for now in range(steps):
            due(now, "then")

        @pl.when(step == steps - 1)
        def _():
            for one in running:
                one.last()

    return pl.pallas_call(
        kernel,
        grid=(steps,),
        out_shape=list(out_shape) + sum(task_outs, []),
        in_specs=list(in_specs) + [anywhere] * len(task_ins),
        out_specs=list(out_specs) + task_out_specs,
        scratch_shapes=scratch,
        compiler_params=pltpu.CompilerParams(
            collective_id=identity, has_side_effects=True, dimension_semantics=("arbitrary",), vmem_limit_bytes=67043328
        ),
        cost_estimate=pl.CostEstimate(flops=flops, bytes_accessed=moved, transcendentals=0),
    )(*operands, *task_ins)


def plain(body, steps, operands, in_specs, out_shape, out_specs, flops, moved):
    return pl.pallas_call(
        body,
        grid=(steps,),
        out_shape=out_shape,
        in_specs=in_specs,
        out_specs=out_specs,
        compiler_params=pltpu.CompilerParams(dimension_semantics=("arbitrary",), vmem_limit_bytes=67043328),
        cost_estimate=pl.CostEstimate(flops=flops, bytes_accessed=moved, transcendentals=0),
    )(*operands)


def by_weight(a, b, tasks=(), identity=None):
    tokens, m = a.shape
    n = b.shape[1]
    rows = m // 16

    def parted(acc, leave_ref, stay_ref):
        core = lax.axis_index("dp") % 2
        first, second = acc[:, 0], acc[:, 1]
        leave_ref[...] = jnp.where(core == 0, second, first).astype(BF16)
        stay_ref[...] = jnp.where(core == 0, first, second)

    if m < n:
        wide, steps = 512, n // 512

        def body(a_ref, b_ref, leave_ref, stay_ref):
            acc = lax.dot_general(a_ref[...], b_ref[...], (((0,), (0,)), ((), ())), preferred_element_type=F32)
            parted(acc.reshape(8, 2, rows, wide), leave_ref, stay_ref)

        specs = [pl.BlockSpec((tokens, m), lambda j: (0, 0)), pl.BlockSpec((tokens, wide), lambda j: (0, j))]
        out = pl.BlockSpec((8, rows, wide), lambda j: (0, 0, j))
    else:
        steps = 8

        def body(a_ref, b_ref, leave_ref, stay_ref):
            acc = lax.dot_general(a_ref[...], b_ref[...], (((0,), (0,)), ((), ())), preferred_element_type=F32)
            parted(acc.reshape(1, 2, rows, n), leave_ref, stay_ref)

        specs = [pl.BlockSpec((tokens, m // 8), lambda j: (0, j)), pl.BlockSpec((tokens, n), lambda j: (0, 0))]
        out = pl.BlockSpec((1, rows, n), lambda j: (j, 0, 0))
    shapes = [jax.ShapeDtypeStruct((8, rows, n), t) for t in (BF16, F32)]
    flops = 2 * tokens * m * n
    if not tasks:
        return plain(body, steps, [a, b], specs, shapes, [out, out], flops, 70 * 2**20)
    return hosting(body, steps, [a, b], specs, shapes, [out, out], tasks, identity, flops, 70 * 2**20)


def gathered(h, tasks, identity):
    tokens, d = h.shape
    tall = 256

    def body(h_ref, a_ref):
        a_ref[...] = normed(h_ref[...])

    row = pl.BlockSpec((tall, d), lambda i: (i, 0))
    like = [jax.ShapeDtypeStruct((tokens, d), BF16)]
    return hosting(body, tokens // tall, [h], [row], like, [row], tasks, identity, 10**9, 10**8)


def hidden(a, w_gate, w_up, tasks, identity):
    tokens, d = a.shape
    ff = w_gate.shape[1]
    wide = 256

    def body(a_ref, gate_w, up_w, gate_ref, up_ref, hid_ref):
        gate = jnp.dot(a_ref[...], gate_w[...], preferred_element_type=F32)
        up = jnp.dot(a_ref[...], up_w[...], preferred_element_type=F32)
        gate_ref[...] = gate
        up_ref[...] = up
        hid_ref[...] = (gate * jax.nn.sigmoid(gate) * up).astype(BF16)

    weight, out = pl.BlockSpec((d, wide), lambda j: (0, j)), pl.BlockSpec((tokens, wide), lambda j: (0, j))
    like = [jax.ShapeDtypeStruct((tokens, ff), t) for t in (F32, F32, BF16)]
    specs = [pl.BlockSpec((tokens, d), lambda j: (0, 0)), weight, weight]
    return hosting(body, ff // wide, [a, w_gate, w_up], specs, like, [out] * 3, tasks, identity, 4 * tokens * d * ff, 150 * 2**20)


def lowered(hid, w_down, h, tasks, identity):
    tokens, ff = hid.shape
    d = w_down.shape[1]
    tall = 256

    def body(hid_ref, w_ref, h_ref, out_ref, a_ref):
        h = h_ref[...] + jnp.dot(hid_ref[...], w_ref[...], preferred_element_type=F32).astype(BF16)
        out_ref[...] = h
        a_ref[...] = normed(h)

    row = pl.BlockSpec((tall, d), lambda i: (i, 0))
    specs = [pl.BlockSpec((tall, ff), lambda i: (i, 0)), pl.BlockSpec((ff, d), lambda i: (0, 0)), row]
    like = [jax.ShapeDtypeStruct((tokens, d), BF16)] * 2
    return hosting(body, tokens // tall, [hid, w_down, h], specs, like, [row] * 2, tasks, identity, 2 * tokens * d * ff, 60 * 2**20)


def unhidden(by, w_down, gate, up, tasks, identity):
    tokens, d = by.shape
    ff = w_down.shape[0]
    wide = 256

    def body(by_ref, w_ref, gate_ref, up_ref, by_gate, by_up):
        by_hid = lax.dot_general(by_ref[...], w_ref[...], (((1,), (1,)), ((), ())), preferred_element_type=F32).astype(BF16).astype(F32)
        gate = gate_ref[...]
        s = jax.nn.sigmoid(gate)
        by_up[...] = (by_hid * (gate * s)).astype(BF16)
        by_gate[...] = (by_hid * up_ref[...] * (s * (1 + gate * (1 - s)))).astype(BF16)

    block = pl.BlockSpec((tokens, wide), lambda j: (0, j))
    like = [jax.ShapeDtypeStruct((tokens, ff), BF16)] * 2
    specs = [pl.BlockSpec((tokens, d), lambda j: (0, 0)), pl.BlockSpec((wide, d), lambda j: (j, 0)), block, block]
    return hosting(body, ff // wide, [by, w_down, gate, up], specs, like, [block] * 2, tasks, identity, 2 * tokens * d * ff, 140 * 2**20)


def by_normed(by_gate, by_up, w_gate, w_up, tasks, identity):
    tokens, ff = by_gate.shape
    d = w_gate.shape[0]
    wide = 256
    steps = ff // wide

    def body(by_gate_ref, by_up_ref, gate_w, up_w, out_ref, total):
        step = pl.program_id(0)
        term = lax.dot_general(by_gate_ref[...], gate_w[...], (((1,), (1,)), ((), ())), preferred_element_type=F32)
        term = term + lax.dot_general(by_up_ref[...], up_w[...], (((1,), (1,)), ((), ())), preferred_element_type=F32)

        @pl.when(step == 0)
        def _():
            total[...] = term

        @pl.when(step > 0)
        def _():
            total[...] += term

        @pl.when(step == steps - 1)
        def _():
            out_ref[...] = total[...].astype(BF16)

    block, weight = pl.BlockSpec((tokens, wide), lambda j: (0, j)), pl.BlockSpec((d, wide), lambda j: (0, j))
    like = [jax.ShapeDtypeStruct((tokens, d), BF16)]
    out = pl.BlockSpec((tokens, d), lambda j: (0, 0))
    flops = 4 * tokens * d * ff
    operands, own = [by_gate, by_up, w_gate, w_up], [pltpu.VMEM((tokens, d), F32)]
    return hosting(body, steps, operands, [block, block, weight, weight], like, [out], tasks, identity, flops, 80 * 2**20, own)


def scattered(parts, identity):
    return hosting(None, 9, [], [], [], [], [(parts, (0, 2, 4, 6))], identity, 10**9, 10**8)


def solution(mesh):
    n = mesh.shape["dp"]
    def step(x, dy, *arrays):
        weights, m, v = (arrays[i : i + 3] for i in (0, 3, 6))
        gate, up, down = ([w] for w in weights)
        h0 = x[0]
        a0, gate_w0, up_w0 = gathered(h0, [(gate, (0, 1, 3, 5), 0), (up, (0, 2, 4, 6), 0)], 1)
        tasks = [(down, (0, 5, 9, 11), 0), (gate, (0, 10, 16, 18), 1)]
        gate0, up0, hid0, down_w0, gate_w1 = hidden(a0, gate_w0, up_w0, tasks, 2)
        h1, a1, up_w1 = lowered(hid0, down_w0, h0, [(up, (0, 4, 7, 7), 1)], 3)
        gate1, up1, hid1, down_w1 = hidden(a1, gate_w1, up_w1, [(down, (0, 6, 11, 14), 1)], 4)

        by = dy[0]
        down1 = list(by_weight(hid1, by))
        by_gate1, by_up1, *g_down1 = unhidden(by, down_w1, gate1, up1, [(down1, (0, 1, 5, 11))], 5)
        in_gate1 = list(by_weight(a1, by_gate1))
        by_a, *g_gate1 = by_normed(by_gate1, by_up1, gate_w1, up_w1, [(in_gate1, (0, 1, 5, 11))], 6)
        by = by + jax.vjp(normed, h1)[1](by_a)[0]
        in_up1 = list(by_weight(a1, by_up1))
        by_gate0, by_up0, *g_up1 = unhidden(by, down_w0, gate0, up0, [(in_up1, (0, 1, 5, 11))], 7)
        down0 = list(by_weight(hid0, by))
        *in_gate0, g_down0, s_down0 = by_weight(a0, by_gate0, [(down0, (0, 1, 4, 8))], 8)
        *in_up0, g_gate0, s_gate0 = by_weight(a0, by_up0, [(in_gate0, (0, 1, 4, 8))], 9)
        g_up0 = scattered(in_up0, 10)

        both = [[(g_gate0, s_gate0), g_gate1], [g_up0, g_up1], [(g_down0, s_down0), g_down1]]
        pairs = [[one[0] for one in pair] for pair in both]
        total = jnp.sum(everywhere(n, sum(one[1] for pair in both for one in pair)))
        count = n * sum(w.size for w in weights)
        factor = jnp.minimum(1.0, 0.5 * lax.rsqrt(total / count + 1e-30))
        new = []
        for w, mm, vv, pair in zip(weights, m, v, pairs, strict=True):
            g = jnp.stack(pair).astype(F32) * factor
            new.append(adamw(w.astype(F32), mm, vv, g))
        return tuple(one[which] for which in range(3) for one in new)

    states, cut = P(("rep", "dp"), None, None), P(None, "dp", None)
    return jax.shard_map(
        step,
        mesh=mesh,
        in_specs=(states, states) + (cut,) * 9,
        out_specs=(P("rep", "dp", None),) * 9,
        check_vma=False,
    )
```

time: 1510 us -> 933 us (0.62)
  Pallas kernels: 0 us -> 886 us
  waiting for transfers between devices: 775 us -> 0 us
  matrix products: 610 us -> 0 us
  blocking collectives: 35.4 us -> 0 us
  local copies, waits for them, and re-layouts: 27.6 us -> 4.95 us
  between operations: 17.6 us -> 1.97 us
    pallas_call x0 -> x15, Pallas kernels: none -> 886 us  [the longest x10 743 us: hosting(): pl.pallas_call(kernel, grid=(steps,), out_shape=list(out_shape) + sum(tas...]
    dot_general x15 -> x0, matrix products: 610 us -> none  [the longest x5 212 us: layer(): gate = jnp.dot(a, w['w_gate'], preferred_element_type=jnp.float32)]
    reduce_scatter x6 -> x0, waiting for transfers between devices: 603 us -> none  [step(): lax.psum_scatter(by_w[name], 'dp', scatter_dimension=0, tiled=True)]
    all_gather x6 -> x0, waiting for transfers between devices: 170 us -> none  [fetched(): lax.all_gather(w[number], 'dp', axis=0, tiled=True)]
    psum x1 -> x0, blocking collectives: 35.4 us -> none  [step(): squares = lax.psum(sum((jnp.sum(g * g) for g in gradients)), 'dp')]
  transfers between devices with their start and end apart: 12 -> 0, of which waited for: 11 -> 0; matrix products, arithmetic and copies ran while one was open for 31% -> 0% of each run, Pallas kernels for 0% -> 0%
where the time goes in v1:
time: 933 us; the launch traced here: 926 us
  Pallas kernels  886 us (95%)
  other arithmetic  32.4 us (3%)
    pallas_call x10, Pallas kernels, hosting(): pl.pallas_call(kernel, grid=(steps,), out_shape=list(out_shape) + sum(tas...  743 us
    pallas_call x4, Pallas kernels, plain(): pl.pallas_call(body, grid=(steps,), out_shape=out_shape, in_specs=in_spec...  136 us

profile of v1, /device:TPU:0, one launch (start us, length us, event | category | flops | bytes accessed | tf_op | source)
XLA Modules:
  0.0 925.5 jit_solution(17808180563910307245)
XLA Ops:
  0.6 92.3 %shard_map.178 = (bf16[2048,1280]{1,0:T(8,128)(2,1)}, bf16[1280,5120]{1,0:T(8,128)(2,1)}, bf16[1280,5120]{1,0:T(8,128)(2,1)}) custom-call(bf16[2048,1280]{1,0:T(8,128)(2,1)} %bitcast.13, bf16[2,80,5120]{2,1,0:T(8,128)(2,1)} %refs_4_.1, bf16[2,80,5120]{2,1,0:T(8,128)(2,1)} %refs_3_.4), custom_call_target="tpu_custom_call" | custom-call | flops 1000000000 | bytes 100000000 | tf_op jit(solution)/shard_map/pallas_call | solution.py:297
  92.9 101.4 %shard_map.179 = (f32[2048,5120]{1,0:T(8,128)}, f32[2048,5120]{1,0:T(8,128)}, bf16[2048,5120]{1,0:T(8,128)(2,1)}, bf16[5120,1280]{1,0:T(8,128)(2,1)}, bf16[1280,5120]{1,0:T(8,128)(2,1)}) custom-call(bf16[2048,1280]{1,0:T(8,128)(2,1)} %get-tuple-element.53.refs_0_, bf16[1280,5120]{1,0:T(8,128)(2,1)} %get-tuple-element.54.refs_1_, ...), custom_call_target="tpu_custom_call" | custom-call | flops 53687091200 | bytes 157286400 | tf_op jit(solution)/shard_map/pallas_call | solution.py:297
  194.3 56.3 %shard_map.180 = (bf16[2048,1280]{1,0:T(8,128)(2,1)}, bf16[2048,1280]{1,0:T(8,128)(2,1)}, bf16[1280,5120]{1,0:T(8,128)(2,1)}) custom-call(bf16[2048,5120]{1,0:T(8,128)(2,1)} %get-tuple-element.56.refs_0_.a_ref, bf16[5120,1280]{1,0:T(8,128)(2,1)} %get-tuple-element.57.refs_1_, bf16[2048,1280]{1,0:T(8,128)(2,1)} %bitcast.14, bf16[2,80,5120]{2,1,0:T(8,128)(2,1)} %refs_3_.4), custom_call_target="tpu_custom_call" | custom-call | flops 26843545600 | bytes 62914560 | tf_op jit(solution)/shard_map/pallas_call | solution.py:297
  250.6 73.0 %shard_map.181 = (f32[2048,5120]{1,0:T(8,128)}, f32[2048,5120]{1,0:T(8,128)}, bf16[2048,5120]{1,0:T(8,128)(2,1)}, bf16[5120,1280]{1,0:T(8,128)(2,1)}) custom-call(bf16[2048,1280]{1,0:T(8,128)(2,1)} %get-tuple-element.58.refs_0_.a_ref, bf16[1280,5120]{1,0:T(8,128)(2,1)} %get-tuple-element.59.refs_1_.refs_2_, ...), custom_call_target="tpu_custom_call" | custom-call | flops 53687091200 | bytes 157286400 | tf_op jit(solution)/shard_map/pallas_call | solution.py:297
  323.6 34.1 %shard_map.182 = (bf16[8,320,1280]{2,1,0:T(8,128)(2,1)}, f32[8,320,1280]{2,1,0:T(8,128)}) custom-call(bf16[2048,5120]{1,0:T(8,128)(2,1)} %get-tuple-element.64.a_ref, bf16[2048,1280]{1,0:T(8,128)(2,1)} %bitcast.11), custom_call_target="tpu_custom_call" | custom-call | flops 26843545600 | bytes 73400320 | tf_op jit(solution)/shard_map/pallas_call | solution.py:312
  357.8 71.4 %shard_map.183 = (bf16[2048,5120]{1,0:T(8,128)(2,1)}, bf16[2048,5120]{1,0:T(8,128)(2,1)}, bf16[320,1280]{1,0:T(8,128)(2,1)}, f32[8,128]{1,0:T(8,128)}) custom-call(bf16[2048,1280]{1,0:T(8,128)(2,1)} %bitcast.12, bf16[5120,1280]{1,0:T(8,128)(2,1)} %get-tuple-element.61.refs_1_, f32[2048,5120]{1,0:T(8,128)} %get-tuple-element.62.refs_2_, ...), custom_call_target="tpu_custom_call" | custom-call | flops 26843545600 | bytes 146800640 | tf_op jit(solution)/shard_map/pallas_call | solution.py:297
  429.2 34.0 %shard_map.184 = (bf16[8,80,5120]{2,1,0:T(8,128)(2,1)}, f32[8,80,5120]{2,1,0:T(8,128)}) custom-call(bf16[2048,1280]{1,0:T(8,128)(2,1)} %get-tuple-element.58.refs_0_.a_ref, bf16[2048,5120]{1,0:T(8,128)(2,1)} %get-tuple-element.67.b_ref.refs_0_), custom_call_target="tpu_custom_call" | custom-call | flops 26843545600 | bytes 73400320 | tf_op jit(solution)/shard_map/pallas_call | solution.py:312
  463.1 91.4 %shard_map.185 = (bf16[2048,1280]{1,0:T(8,128)(2,1)}, bf16[80,5120]{1,0:T(8,128)(2,1)}, f32[8,128]{1,0:T(8,128)}) custom-call(bf16[2048,5120]{1,0:T(8,128)(2,1)} %get-tuple-element.67.b_ref.refs_0_, bf16[2048,5120]{1,0:T(8,128)(2,1)} %get-tuple-element.68.refs_1_.b_ref, bf16[1280,5120]{1,0:T(8,128)(2,1)} %get-tuple-element.59.refs_1_.refs_2_, ...), custom_call_target="tpu_custom_call" | custom-call | flops 53687091200 | bytes 83886080 | tf_op jit(solution)/shard_map/pallas_call | solution.py:297
  554.6 34.0 %shard_map.186 = (bf16[8,80,5120]{2,1,0:T(8,128)(2,1)}, f32[8,80,5120]{2,1,0:T(8,128)}) custom-call(bf16[2048,1280]{1,0:T(8,128)(2,1)} %get-tuple-element.58.refs_0_.a_ref, bf16[2048,5120]{1,0:T(8,128)(2,1)} %get-tuple-element.68.refs_1_.b_ref), custom_call_target="tpu_custom_call" | custom-call | flops 26843545600 | bytes 73400320 | tf_op jit(solution)/shard_map/pallas_call | solution.py:312
  588.6 0.0 slice-start
  588.6 0.0 slice-start.1
  588.6 0.0 copy-start
  588.6 6.3 fusion.2
  594.9 0.0 slice-done
  594.9 0.0 slice-done.1
  594.9 0.7 copy-done
  595.7 7.1 fusion.4.refs_0_.b_ref
  602.8 70.8 %shard_map.187 = (bf16[2048,5120]{1,0:T(8,128)(2,1)}, bf16[2048,5120]{1,0:T(8,128)(2,1)}, bf16[80,5120]{1,0:T(8,128)(2,1)}, f32[8,128]{1,0:T(8,128)}) custom-call(bf16[2048,1280]{1,0:T(8,128)(2,1)} %fusion.4.refs_0_.b_ref, bf16[5120,1280]{1,0:T(8,128)(2,1)} %get-tuple-element.57.refs_1_, f32[2048,5120]{1,0:T(8,128)} %get-tuple-element.73.refs_2_, ...), custom_call_target="tpu_custom_call" | custom-call | flops 26843545600 | bytes 146800640 | tf_op jit(solution)/shard_map/pallas_call | solution.py:297
  673.6 33.7 %shard_map.188 = (bf16[8,320,1280]{2,1,0:T(8,128)(2,1)}, f32[8,320,1280]{2,1,0:T(8,128)}) custom-call(bf16[2048,5120]{1,0:T(8,128)(2,1)} %get-tuple-element.56.refs_0_.a_ref, bf16[2048,1280]{1,0:T(8,128)(2,1)} %fusion.4.refs_0_.b_ref), custom_call_target="tpu_custom_call" | custom-call | flops 26843545600 | bytes 73400320 | tf_op jit(solution)/shard_map/pallas_call | solution.py:312
  707.3 65.0 %shard_map.189 = (bf16[8,80,5120]{2,1,0:T(8,128)(2,1)}, f32[8,80,5120]{2,1,0:T(8,128)}, bf16[320,1280]{1,0:T(8,128)(2,1)}, f32[8,128]{1,0:T(8,128)}) custom-call(bf16[2048,1280]{1,0:T(8,128)(2,1)} %get-tuple-element.53.refs_0_, bf16[2048,5120]{1,0:T(8,128)(2,1)} %get-tuple-element.78.refs_1_, bf16[8,320,1280]{2,1,0:T(8,128)(2,1)} %get-tuple-element.79.refs_2_, ...), custom_call_target="tpu_custom_call" | custom-call | flops 26843545600 | bytes 73400320 | tf_op jit(solution)/shard_map/pallas_call | solution.py:297
  772.3 67.8 %shard_map.190 = (bf16[8,80,5120]{2,1,0:T(8,128)(2,1)}, f32[8,80,5120]{2,1,0:T(8,128)}, bf16[80,5120]{1,0:T(8,128)(2,1)}, f32[8,128]{1,0:T(8,128)}) custom-call(bf16[2048,1280]{1,0:T(8,128)(2,1)} %get-tuple-element.53.refs_0_, bf16[2048,5120]{1,0:T(8,128)(2,1)} %get-tuple-element.77.refs_1_, bf16[8,80,5120]{2,1,0:T(8,128)(2,1)} %get-tuple-element.81.refs_2_, ...), custom_call_target="tpu_custom_call" | custom-call | flops 26843545600 | bytes 73400320 | tf_op jit(solution)/shard_map/pallas_call | solution.py:297
  840.1 54.0 %shard_map.191 = (bf16[80,5120]{1,0:T(8,128)(2,1)}, f32[8,128]{1,0:T(8,128)}) custom-call(bf16[8,80,5120]{2,1,0:T(8,128)(2,1)} %get-tuple-element.87.refs_0_, f32[8,80,5120]{2,1,0:T(8,128)} %get-tuple-element.88.refs_1_), custom_call_target="tpu_custom_call" | custom-call | flops 1000000000 | bytes 100000000 | tf_op jit(solution)/shard_map/pallas_call | solution.py:297
  894.1 1.3 add_add_fusion.part_ref
  895.4 7.0 shard_map.192
  902.5 1.3 reduce_sum.33
  904.4 0.0 copy-start.1
  904.5 0.0 copy-start.2
  904.5 0.0 copy-start.3
  904.5 0.0 copy-start.4
  904.5 0.0 copy-start.5
  904.5 0.0 copy-start.6
  904.5 0.0 copy-start.7
  904.5 0.0 copy-start.8
  904.5 7.6 fusion.13
  912.2 0.0 copy-done.1
  912.2 0.0 copy-done.2
  912.2 1.0 copy-done.3
  913.1 1.0 copy-done.4
  914.1 0.9 copy-done.5
  915.0 0.9 copy-done.6
  916.0 0.1 copy-done.7
  916.1 0.2 copy-done.8
  916.3 8.7 fusion.7
  (2 shorter events, 0.0 us)
Async XLA Ops:
  588.6 6.4 slice-start
  588.6 6.4 slice-start.1
  588.6 7.1 copy-start
  904.4 7.7 copy-start.1
  904.5 7.7 copy-start.2
  904.5 8.7 copy-start.3
  904.5 9.6 %copy-start.4 = (f32[2,80,5120]{2,1,0:T(8,128)S(1)}, f32[2,80,5120]{2,1,0:T(8,128)}, u32[]{:S(2)}) copy-start(f32[2,80,5120]{2,1,0:T(8,128)} %param.16) | copy-start | bytes 9830404
  904.5 10.5 %copy-start.5 = (f32[2,80,5120]{2,1,0:T(8,128)S(1)}, f32[2,80,5120]{2,1,0:T(8,128)}, u32[]{:S(2)}) copy-start(f32[2,80,5120]{2,1,0:T(8,128)} %param.20) | copy-start | bytes 9830404
  904.5 11.5 %copy-start.6 = (f32[2,80,5120]{2,1,0:T(8,128)S(1)}, f32[2,80,5120]{2,1,0:T(8,128)}, u32[]{:S(2)}) copy-start(f32[2,80,5120]{2,1,0:T(8,128)} %param.17) | copy-start | bytes 9830404
  904.5 11.6 %copy-start.7 = (bf16[80,5120]{1,0:T(8,128)(2,1)S(1)}, bf16[80,5120]{1,0:T(8,128)(2,1)}, u32[]{:S(2)}) copy-start(bf16[80,5120]{1,0:T(8,128)(2,1)} %get-tuple-element.84) | copy-start | bytes 2457604
  904.5 11.8 %copy-start.8 = (bf16[80,5120]{1,0:T(8,128)(2,1)S(1)}, bf16[80,5120]{1,0:T(8,128)(2,1)}, u32[]{:S(2)}) copy-start(bf16[80,5120]{1,0:T(8,128)(2,1)} %get-tuple-element.94) | copy-start | bytes 2457604

commit v2 on v1

--- a/solution.py
+++ b/solution.py
@@ -102,10 +102,7 @@
         self.near = [copy(9 + k, bits, 1) for k, bits in enumerate(self.HANDED)]
         self.local = pltpu.make_async_copy(shard, block(0), local_sem)
 
-    def then(self, phase):
-        pass
-
-    def before(self, number):
+    def start(self, number):
         if number == 0:
             for copy in self.far[:3] + self.near[:1] + [self.local]:
                 copy.start()
@@ -182,11 +179,12 @@
         self.near[k].wait_recv()
         self.loads[k].wait()
 
-    def before(self, phase):
+    def start(self, phase):
         if phase == 0:
             for one in self.near + self.loads:
                 one.start()
-            return
+
+    def sum(self, phase):
         stage = phase - 1
         for m in self.SUMS[stage]:
             self.ready(m)
@@ -209,10 +207,9 @@
 
             lax.fori_loop(0, self.rows // 16, add, 0)
 
-    def then(self, phase):
-        if phase:
-            for copy in self.far[phase - 1]:
-                copy.start()
+    def send(self, phase):
+        for copy in self.far[phase - 1]:
+            copy.start()
 
     def last(self):
         self.ready(0)
@@ -236,7 +233,7 @@
             copy.wait_send()
 
 
-def hosting(body, steps, operands, in_specs, out_shape, out_specs, tasks, identity, flops, moved, own_scratch=()):
+def hosting(body, steps, operands, in_specs, out_shape, out_specs, tasks, identity, flops, moved, own_scratch=(), idle=0):
     given, made = len(operands), len(out_shape)
     anywhere = pl.BlockSpec(memory_space=pl.ANY)
     task_ins, task_outs, task_out_specs, scratch, shape_of = [], [], [], [], []
@@ -270,24 +267,34 @@
             running.append((Gather if n == 1 else Scatter)(*mine, *out, *take(k)))
         step = pl.program_id(0)
 
-        def due(now, action):
-            wait = 1 if body is None and action == "then" else 0
-            todo = sorted((phase, i) for i, (_, when, *_) in enumerate(tasks) for phase in range(4) if when[phase] + wait == now)
+        def due(now, early):
+            todo = []
+            for i, ((arrays, when, *_), one) in enumerate(zip(tasks, running, strict=True)):
+                for phase in range(4):
+                    if len(arrays) == 1 or phase == 0:
+                        todo += [(phase, i, one.start)] if early and when[phase] == now else []
+                    elif early:
+                        todo += [(phase, i, one.send)] if when[phase] + 1 == now else []
+                    else:
+                        todo += [(phase, i, one.sum)] if when[phase] == now else []
             if todo:
 
                 @pl.when(step == now)
                 def _():
-                    if now == 0 and action == "before":
+                    if now == 0 and early:
                         meet()
-                    for phase, i in todo:
-                        getattr(running[i], action)(phase)
+                    for phase, _, action in sorted(todo, key=lambda one: one[:2]):
+                        action(phase)
 
         for now in range(steps):
-            due(now, "before")
+            due(now, True)
         if body is not None:
-            body(*ins, *outs, *refs)
+            if idle:
+                pl.when(step < steps - idle)(lambda: body(*ins, *outs, *refs))
+            else:
+                body(*ins, *outs, *refs)
         for now in range(steps):
-            due(now, "then")
+            due(now, False)
 
         @pl.when(step == steps - 1)
         def _():
@@ -331,29 +338,33 @@
         leave_ref[...] = jnp.where(core == 0, second, first).astype(BF16)
         stay_ref[...] = jnp.where(core == 0, first, second)
 
+    idle = 2 if tasks else 0
+    wide, real = 512, n // 512 if m < n else 8
+
+    def at(j):
+        return j - j // real * (j - real + 1)
+
     if m < n:
-        wide, steps = 512, n // 512
 
         def body(a_ref, b_ref, leave_ref, stay_ref):
             acc = lax.dot_general(a_ref[...], b_ref[...], (((0,), (0,)), ((), ())), preferred_element_type=F32)
             parted(acc.reshape(8, 2, rows, wide), leave_ref, stay_ref)
 
-        specs = [pl.BlockSpec((tokens, m), lambda j: (0, 0)), pl.BlockSpec((tokens, wide), lambda j: (0, j))]
-        out = pl.BlockSpec((8, rows, wide), lambda j: (0, 0, j))
+        specs = [pl.BlockSpec((tokens, m), lambda j: (0, 0)), pl.BlockSpec((tokens, wide), lambda j: (0, at(j)))]
+        out = pl.BlockSpec((8, rows, wide), lambda j: (0, 0, at(j)))
     else:
-        steps = 8
 
         def body(a_ref, b_ref, leave_ref, stay_ref):
             acc = lax.dot_general(a_ref[...], b_ref[...], (((0,), (0,)), ((), ())), preferred_element_type=F32)
             parted(acc.reshape(1, 2, rows, n), leave_ref, stay_ref)
 
-        specs = [pl.BlockSpec((tokens, m // 8), lambda j: (0, j)), pl.BlockSpec((tokens, n), lambda j: (0, 0))]
-        out = pl.BlockSpec((1, rows, n), lambda j: (j, 0, 0))
+        specs = [pl.BlockSpec((tokens, m // 8), lambda j: (0, at(j))), pl.BlockSpec((tokens, n), lambda j: (0, 0))]
+        out = pl.BlockSpec((1, rows, n), lambda j: (at(j), 0, 0))
     shapes = [jax.ShapeDtypeStruct((8, rows, n), t) for t in (BF16, F32)]
     flops = 2 * tokens * m * n
     if not tasks:
-        return plain(body, steps, [a, b], specs, shapes, [out, out], flops, 70 * 2**20)
-    return hosting(body, steps, [a, b], specs, shapes, [out, out], tasks, identity, flops, 70 * 2**20)
+        return plain(body, real, [a, b], specs, shapes, [out, out], flops, 70 * 2**20)
+    return hosting(body, real + idle, [a, b], specs, shapes, [out, out], tasks, identity, flops, 70 * 2**20, idle=idle)
 
 
 def gathered(h, tasks, identity):
@@ -368,10 +379,14 @@
     return hosting(body, tokens // tall, [h], [row], like, [row], tasks, identity, 10**9, 10**8)
 
 
-def hidden(a, w_gate, w_up, tasks, identity):
+def hidden(a, w_gate, w_up, tasks, identity, idle=0):
     tokens, d = a.shape
     ff = w_gate.shape[1]
     wide = 256
+    real = ff // wide
+
+    def at(j):
+        return j - j // real * (j - real + 1)
 
     def body(a_ref, gate_w, up_w, gate_ref, up_ref, hid_ref):
         gate = jnp.dot(a_ref[...], gate_w[...], preferred_element_type=F32)
@@ -380,26 +395,36 @@
         up_ref[...] = up
         hid_ref[...] = (gate * jax.nn.sigmoid(gate) * up).astype(BF16)
 
-    weight, out = pl.BlockSpec((d, wide), lambda j: (0, j)), pl.BlockSpec((tokens, wide), lambda j: (0, j))
+    weight, out = pl.BlockSpec((d, wide), lambda j: (0, at(j))), pl.BlockSpec((tokens, wide), lambda j: (0, at(j)))
     like = [jax.ShapeDtypeStruct((tokens, ff), t) for t in (F32, F32, BF16)]
     specs = [pl.BlockSpec((tokens, d), lambda j: (0, 0)), weight, weight]
-    return hosting(body, ff // wide, [a, w_gate, w_up], specs, like, [out] * 3, tasks, identity, 4 * tokens * d * ff, 150 * 2**20)
+    return hosting(body, real + idle, [a, w_gate, w_up], specs, like, [out] * 3, tasks, identity, 4 * tokens * d * ff, 150 * 2**20, idle=idle)
 
 
 def lowered(hid, w_down, h, tasks, identity):
     tokens, ff = hid.shape
     d = w_down.shape[1]
-    tall = 256
-
-    def body(hid_ref, w_ref, h_ref, out_ref, a_ref):
-        h = h_ref[...] + jnp.dot(hid_ref[...], w_ref[...], preferred_element_type=F32).astype(BF16)
+    tall, idle = 256, 2
+    real = tokens // tall
+
+    def at(i):
+        return i - i // real * (i - real + 1)
+
+    def body(hid_ref, w_ref, h_ref, out_ref, a_ref, held, sem):
+        @pl.when(pl.program_id(0) == 0)
+        def _():
+            copy = pltpu.make_async_copy(w_ref, held, sem)
+            copy.start()
+            copy.wait()
+
+        h = h_ref[...] + jnp.dot(hid_ref[...], held[...], preferred_element_type=F32).astype(BF16)
         out_ref[...] = h
         a_ref[...] = normed(h)
 
-    row = pl.BlockSpec((tall, d), lambda i: (i, 0))
-    specs = [pl.BlockSpec((tall, ff), lambda i: (i, 0)), pl.BlockSpec((ff, d), lambda i: (0, 0)), row]
+    row = pl.BlockSpec((tall, d), lambda i: (at(i), 0))
+    specs = [pl.BlockSpec((tall, ff), lambda i: (at(i), 0)), pl.BlockSpec(memory_space=pl.ANY), row]
     like = [jax.ShapeDtypeStruct((tokens, d), BF16)] * 2
-    return hosting(body, tokens // tall, [hid, w_down, h], specs, like, [row] * 2, tasks, identity, 2 * tokens * d * ff, 60 * 2**20)
+    return hosting(body, real + idle, [hid, w_down, h], specs, like, [row] * 2, tasks, identity, 2 * tokens * d * ff, 60 * 2**20, [pltpu.VMEM((ff, d), BF16), pltpu.SemaphoreType.DMA(())], idle)
 
 
 def unhidden(by, w_down, gate, up, tasks, identity):
@@ -428,16 +453,11 @@
 
     def body(by_gate_ref, by_up_ref, gate_w, up_w, out_ref, total):
         step = pl.program_id(0)
-        term = lax.dot_general(by_gate_ref[...], gate_w[...], (((1,), (1,)), ((), ())), preferred_element_type=F32)
-        term = term + lax.dot_general(by_up_ref[...], up_w[...], (((1,), (1,)), ((), ())), preferred_element_type=F32)
-
-        @pl.when(step == 0)
-        def _():
-            total[...] = term
-
-        @pl.when(step > 0)
-        def _():
-            total[...] += term
+        for start in range(0, tokens, 512):
+            some = pl.ds(start, 512)
+            term = lax.dot_general(by_gate_ref[some, :], gate_w[...], (((1,), (1,)), ((), ())), preferred_element_type=F32)
+            term = term + lax.dot_general(by_up_ref[some, :], up_w[...], (((1,), (1,)), ((), ())), preferred_element_type=F32)
+            total[some, :] = jnp.where(step > 0, total[some, :], 0.0) + term
 
         @pl.when(step == steps - 1)
         def _():
@@ -452,7 +472,7 @@
 
 
 def scattered(parts, identity):
-    return hosting(None, 9, [], [], [], [], [(parts, (0, 2, 4, 6))], identity, 10**9, 10**8)
+    return hosting(None, 6, [], [], [], [], [(parts, (0, 0, 2, 4))], identity, 10**9, 10**8)
 
 
 def solution(mesh):
@@ -462,22 +482,22 @@
         gate, up, down = ([w] for w in weights)
         h0 = x[0]
         a0, gate_w0, up_w0 = gathered(h0, [(gate, (0, 1, 3, 5), 0), (up, (0, 2, 4, 6), 0)], 1)
-        tasks = [(down, (0, 5, 9, 11), 0), (gate, (0, 10, 16, 18), 1)]
-        gate0, up0, hid0, down_w0, gate_w1 = hidden(a0, gate_w0, up_w0, tasks, 2)
-        h1, a1, up_w1 = lowered(hid0, down_w0, h0, [(up, (0, 4, 7, 7), 1)], 3)
+        tasks = [(down, (0, 6, 16, 20), 0), (gate, (0, 11, 20, 21), 1)]
+        gate0, up0, hid0, down_w0, gate_w1 = hidden(a0, gate_w0, up_w0, tasks, 2, 2)
+        h1, a1, up_w1 = lowered(hid0, down_w0, h0, [(up, (0, 3, 8, 9), 1)], 3)
         gate1, up1, hid1, down_w1 = hidden(a1, gate_w1, up_w1, [(down, (0, 6, 11, 14), 1)], 4)
 
         by = dy[0]
         down1 = list(by_weight(hid1, by))
-        by_gate1, by_up1, *g_down1 = unhidden(by, down_w1, gate1, up1, [(down1, (0, 1, 5, 11))], 5)
+        by_gate1, by_up1, *g_down1 = unhidden(by, down_w1, gate1, up1, [(down1, (0, 0, 3, 11))], 5)
         in_gate1 = list(by_weight(a1, by_gate1))
-        by_a, *g_gate1 = by_normed(by_gate1, by_up1, gate_w1, up_w1, [(in_gate1, (0, 1, 5, 11))], 6)
+        by_a, *g_gate1 = by_normed(by_gate1, by_up1, gate_w1, up_w1, [(in_gate1, (0, 0, 3, 9))], 6)
         by = by + jax.vjp(normed, h1)[1](by_a)[0]
         in_up1 = list(by_weight(a1, by_up1))
-        by_gate0, by_up0, *g_up1 = unhidden(by, down_w0, gate0, up0, [(in_up1, (0, 1, 5, 11))], 7)
+        by_gate0, by_up0, *g_up1 = unhidden(by, down_w0, gate0, up0, [(in_up1, (0, 0, 3, 11))], 7)
         down0 = list(by_weight(hid0, by))
-        *in_gate0, g_down0, s_down0 = by_weight(a0, by_gate0, [(down0, (0, 1, 4, 8))], 8)
-        *in_up0, g_gate0, s_gate0 = by_weight(a0, by_up0, [(in_gate0, (0, 1, 4, 8))], 9)
+        *in_gate0, g_down0, s_down0 = by_weight(a0, by_gate0, [(down0, (0, 0, 3, 9))], 8)
+        *in_up0, g_gate0, s_gate0 = by_weight(a0, by_up0, [(in_gate0, (0, 0, 3, 9))], 9)
         g_up0 = scattered(in_up0, 10)
 
         both = [[(g_gate0, s_gate0), g_gate1], [g_up0, g_up1], [(g_down0, s_down0), g_down1]]

time: 933 us -> 878 us (0.941)
  Pallas kernels: 886 us -> 831 us
    pallas_call x10, Pallas kernels: 743 us -> 688 us  [hosting(): pl.pallas_call(kernel, grid=(steps,), out_shape=list(out_shape) + sum(tas...]
where the time goes in v2:
time: 878 us; the launch traced here: 870 us
  Pallas kernels  831 us (95%)
  other arithmetic  32.4 us (4%)
    pallas_call x10, Pallas kernels, hosting(): pl.pallas_call(kernel, grid=(steps,), out_shape=list(out_shape) + sum(tas...  688 us
    pallas_call x4, Pallas kernels, plain(): pl.pallas_call(body, grid=(steps,), out_shape=out_shape, in_specs=in_spec...  136 us

profile of v2, /device:TPU:0, one launch (start us, length us, event | category | flops | bytes accessed | tf_op | source)
XLA Modules:
  0.0 870.4 jit_solution(6655417846319632327)
XLA Ops:
  0.6 92.3 %shard_map.178 = (bf16[2048,1280]{1,0:T(8,128)(2,1)}, bf16[1280,5120]{1,0:T(8,128)(2,1)}, bf16[1280,5120]{1,0:T(8,128)(2,1)}) custom-call(bf16[2048,1280]{1,0:T(8,128)(2,1)} %bitcast.13, bf16[2,80,5120]{2,1,0:T(8,128)(2,1)} %refs_4_.1, bf16[2,80,5120]{2,1,0:T(8,128)(2,1)} %refs_3_.4), custom_call_target="tpu_custom_call" | custom-call | flops 1000000000 | bytes 100000000 | tf_op jit(solution)/shard_map/pallas_call | solution.py:304
  92.9 94.4 %shard_map.179 = (f32[2048,5120]{1,0:T(8,128)}, f32[2048,5120]{1,0:T(8,128)}, bf16[2048,5120]{1,0:T(8,128)(2,1)}, bf16[5120,1280]{1,0:T(8,128)(2,1)}, bf16[1280,5120]{1,0:T(8,128)(2,1)}) custom-call(bf16[2048,1280]{1,0:T(8,128)(2,1)} %get-tuple-element.53.refs_0_, bf16[1280,5120]{1,0:T(8,128)(2,1)} %get-tuple-element.54.refs_1_, ...), custom_call_target="tpu_custom_call" | custom-call | flops 53687091200 | bytes 157286400 | tf_op jit(solution)/shard_map/pallas_call | solution.py:304
  187.4 53.2 %shard_map.180 = (bf16[2048,1280]{1,0:T(8,128)(2,1)}, bf16[2048,1280]{1,0:T(8,128)(2,1)}, bf16[1280,5120]{1,0:T(8,128)(2,1)}) custom-call(bf16[2048,5120]{1,0:T(8,128)(2,1)} %get-tuple-element.56.refs_0_.a_ref, bf16[5120,1280]{1,0:T(8,128)(2,1)} %get-tuple-element.57.refs_1_, bf16[2048,1280]{1,0:T(8,128)(2,1)} %bitcast.14, bf16[2,80,5120]{2,1,0:T(8,128)(2,1)} %refs_3_.4), custom_call_target="tpu_custom_call" | custom-call | flops 26843545600 | bytes 62914560 | tf_op jit(solution)/shard_map/pallas_call | solution.py:304
  240.6 73.3 %shard_map.181 = (f32[2048,5120]{1,0:T(8,128)}, f32[2048,5120]{1,0:T(8,128)}, bf16[2048,5120]{1,0:T(8,128)(2,1)}, bf16[5120,1280]{1,0:T(8,128)(2,1)}) custom-call(bf16[2048,1280]{1,0:T(8,128)(2,1)} %get-tuple-element.58.refs_0_.a_ref, bf16[1280,5120]{1,0:T(8,128)(2,1)} %get-tuple-element.59.refs_1_.refs_2_, ...), custom_call_target="tpu_custom_call" | custom-call | flops 53687091200 | bytes 157286400 | tf_op jit(solution)/shard_map/pallas_call | solution.py:304
  313.9 33.9 %shard_map.182 = (bf16[8,320,1280]{2,1,0:T(8,128)(2,1)}, f32[8,320,1280]{2,1,0:T(8,128)}) custom-call(bf16[2048,5120]{1,0:T(8,128)(2,1)} %get-tuple-element.64.a_ref, bf16[2048,1280]{1,0:T(8,128)(2,1)} %bitcast.11), custom_call_target="tpu_custom_call" | custom-call | flops 26843545600 | bytes 73400320 | tf_op jit(solution)/shard_map/pallas_call | solution.py:319
  347.8 65.3 %shard_map.183 = (bf16[2048,5120]{1,0:T(8,128)(2,1)}, bf16[2048,5120]{1,0:T(8,128)(2,1)}, bf16[320,1280]{1,0:T(8,128)(2,1)}, f32[8,128]{1,0:T(8,128)}) custom-call(bf16[2048,1280]{1,0:T(8,128)(2,1)} %bitcast.12, bf16[5120,1280]{1,0:T(8,128)(2,1)} %get-tuple-element.61.refs_1_, f32[2048,5120]{1,0:T(8,128)} %get-tuple-element.62.refs_2_, ...), custom_call_target="tpu_custom_call" | custom-call | flops 26843545600 | bytes 146800640 | tf_op jit(solution)/shard_map/pallas_call | solution.py:304
  413.1 34.1 %shard_map.184 = (bf16[8,80,5120]{2,1,0:T(8,128)(2,1)}, f32[8,80,5120]{2,1,0:T(8,128)}) custom-call(bf16[2048,1280]{1,0:T(8,128)(2,1)} %get-tuple-element.58.refs_0_.a_ref, bf16[2048,5120]{1,0:T(8,128)(2,1)} %get-tuple-element.67.b_ref.refs_0_), custom_call_target="tpu_custom_call" | custom-call | flops 26843545600 | bytes 73400320 | tf_op jit(solution)/shard_map/pallas_call | solution.py:319
  447.2 71.8 %shard_map.185 = (bf16[2048,1280]{1,0:T(8,128)(2,1)}, bf16[80,5120]{1,0:T(8,128)(2,1)}, f32[8,128]{1,0:T(8,128)}) custom-call(bf16[2048,5120]{1,0:T(8,128)(2,1)} %get-tuple-element.67.b_ref.refs_0_, bf16[2048,5120]{1,0:T(8,128)(2,1)} %get-tuple-element.68.refs_1_.b_ref, bf16[1280,5120]{1,0:T(8,128)(2,1)} %get-tuple-element.59.refs_1_.refs_2_, ...), custom_call_target="tpu_custom_call" | custom-call | flops 53687091200 | bytes 83886080 | tf_op jit(solution)/shard_map/pallas_call | solution.py:304
  519.1 34.4 %shard_map.186 = (bf16[8,80,5120]{2,1,0:T(8,128)(2,1)}, f32[8,80,5120]{2,1,0:T(8,128)}) custom-call(bf16[2048,1280]{1,0:T(8,128)(2,1)} %get-tuple-element.58.refs_0_.a_ref, bf16[2048,5120]{1,0:T(8,128)(2,1)} %get-tuple-element.68.refs_1_.b_ref), custom_call_target="tpu_custom_call" | custom-call | flops 26843545600 | bytes 73400320 | tf_op jit(solution)/shard_map/pallas_call | solution.py:319
  553.4 0.0 slice-start
  553.4 0.0 slice-start.1
  553.4 0.0 copy-start
  553.4 6.3 fusion.2
  559.8 0.0 slice-done
  559.8 0.0 slice-done.1
  559.8 0.7 copy-done
  560.5 7.1 fusion.4.refs_0_.b_ref
  567.6 64.7 %shard_map.187 = (bf16[2048,5120]{1,0:T(8,128)(2,1)}, bf16[2048,5120]{1,0:T(8,128)(2,1)}, bf16[80,5120]{1,0:T(8,128)(2,1)}, f32[8,128]{1,0:T(8,128)}) custom-call(bf16[2048,1280]{1,0:T(8,128)(2,1)} %fusion.4.refs_0_.b_ref, bf16[5120,1280]{1,0:T(8,128)(2,1)} %get-tuple-element.57.refs_1_, f32[2048,5120]{1,0:T(8,128)} %get-tuple-element.73.refs_2_, ...), custom_call_target="tpu_custom_call" | custom-call | flops 26843545600 | bytes 146800640 | tf_op jit(solution)/shard_map/pallas_call | solution.py:304
  632.4 33.8 %shard_map.188 = (bf16[8,320,1280]{2,1,0:T(8,128)(2,1)}, f32[8,320,1280]{2,1,0:T(8,128)}) custom-call(bf16[2048,5120]{1,0:T(8,128)(2,1)} %get-tuple-element.56.refs_0_.a_ref, bf16[2048,1280]{1,0:T(8,128)(2,1)} %fusion.4.refs_0_.b_ref), custom_call_target="tpu_custom_call" | custom-call | flops 26843545600 | bytes 73400320 | tf_op jit(solution)/shard_map/pallas_call | solution.py:319
  666.2 60.1 %shard_map.189 = (bf16[8,80,5120]{2,1,0:T(8,128)(2,1)}, f32[8,80,5120]{2,1,0:T(8,128)}, bf16[320,1280]{1,0:T(8,128)(2,1)}, f32[8,128]{1,0:T(8,128)}) custom-call(bf16[2048,1280]{1,0:T(8,128)(2,1)} %get-tuple-element.53.refs_0_, bf16[2048,5120]{1,0:T(8,128)(2,1)} %get-tuple-element.78.refs_1_, bf16[8,320,1280]{2,1,0:T(8,128)(2,1)} %get-tuple-element.79.refs_2_, ...), custom_call_target="tpu_custom_call" | custom-call | flops 26843545600 | bytes 73400320 | tf_op jit(solution)/shard_map/pallas_call | solution.py:304
  726.3 59.2 %shard_map.190 = (bf16[8,80,5120]{2,1,0:T(8,128)(2,1)}, f32[8,80,5120]{2,1,0:T(8,128)}, bf16[80,5120]{1,0:T(8,128)(2,1)}, f32[8,128]{1,0:T(8,128)}) custom-call(bf16[2048,1280]{1,0:T(8,128)(2,1)} %get-tuple-element.53.refs_0_, bf16[2048,5120]{1,0:T(8,128)(2,1)} %get-tuple-element.77.refs_1_, bf16[8,80,5120]{2,1,0:T(8,128)(2,1)} %get-tuple-element.81.refs_2_, ...), custom_call_target="tpu_custom_call" | custom-call | flops 26843545600 | bytes 73400320 | tf_op jit(solution)/shard_map/pallas_call | solution.py:304
  785.5 53.5 %shard_map.191 = (bf16[80,5120]{1,0:T(8,128)(2,1)}, f32[8,128]{1,0:T(8,128)}) custom-call(bf16[8,80,5120]{2,1,0:T(8,128)(2,1)} %get-tuple-element.87.refs_0_, f32[8,80,5120]{2,1,0:T(8,128)} %get-tuple-element.88.refs_1_), custom_call_target="tpu_custom_call" | custom-call | flops 1000000000 | bytes 100000000 | tf_op jit(solution)/shard_map/pallas_call | solution.py:304
  839.0 1.3 add_add_fusion.part_ref
  840.3 7.0 shard_map.192
  847.3 1.3 reduce_sum.33
  849.3 0.0 copy-start.1
  849.3 0.0 copy-start.2
  849.3 0.0 copy-start.3
  849.3 0.0 copy-start.4
  849.4 0.0 copy-start.5
  849.4 0.0 copy-start.6
  849.4 0.0 copy-start.7
  849.4 0.0 copy-start.8
  849.4 7.6 fusion.13
  857.0 0.0 copy-done.1
  857.0 0.0 copy-done.2
  857.0 1.0 copy-done.3
  858.0 1.0 copy-done.4
  859.0 0.9 copy-done.5
  859.9 0.9 copy-done.6
  860.8 0.1 copy-done.7
  861.0 0.2 copy-done.8
  861.2 8.7 %fusion.7 = (bf16[2,80,5120]{2,1,0:T(8,128)(2,1)}, f32[2,80,5120]{2,1,0:T(8,128)}, f32[2,80,5120]{2,1,0:T(8,128)}, bf16[2,80,5120]{2,1,0:T(8,128)(2,1)}, f32[2,80,5120]{2,1,0:T(8,128)}, /*index=5*/f32[2,80,5120]{2,1,0:T(8,128)}) fusion(bf16[2,80,5120]{2,1,0:T(8,128)(2,1)S(1)} %copy-done.1, f32[]{:T(128)S(6)} %min_shard_map.3, ...), kind=kLoop, calls=%fused_computation.20 | loop fusion | flops 32768000 | bytes 36044804 | tf_op jit(solution)/shard_map/convert_element_type | solution.py:21
  (2 shorter events, 0.0 us)
Async XLA Ops:
  553.4 6.4 slice-start
  553.4 6.4 slice-start.1
  553.4 7.1 copy-start
  849.3 7.7 copy-start.1
  849.3 7.7 copy-start.2
  849.3 8.7 copy-start.3
  849.3 9.6 %copy-start.4 = (f32[2,80,5120]{2,1,0:T(8,128)S(1)}, f32[2,80,5120]{2,1,0:T(8,128)}, u32[]{:S(2)}) copy-start(f32[2,80,5120]{2,1,0:T(8,128)} %param.16) | copy-start | bytes 9830404
  849.4 10.5 %copy-start.5 = (f32[2,80,5120]{2,1,0:T(8,128)S(1)}, f32[2,80,5120]{2,1,0:T(8,128)}, u32[]{:S(2)}) copy-start(f32[2,80,5120]{2,1,0:T(8,128)} %param.20) | copy-start | bytes 9830404
  849.4 11.5 %copy-start.6 = (f32[2,80,5120]{2,1,0:T(8,128)S(1)}, f32[2,80,5120]{2,1,0:T(8,128)}, u32[]{:S(2)}) copy-start(f32[2,80,5120]{2,1,0:T(8,128)} %param.17) | copy-start | bytes 9830404
  849.4 11.6 %copy-start.7 = (bf16[80,5120]{1,0:T(8,128)(2,1)S(1)}, bf16[80,5120]{1,0:T(8,128)(2,1)}, u32[]{:S(2)}) copy-start(bf16[80,5120]{1,0:T(8,128)(2,1)} %get-tuple-element.84) | copy-start | bytes 2457604
  849.4 11.8 %copy-start.8 = (bf16[80,5120]{1,0:T(8,128)(2,1)S(1)}, bf16[80,5120]{1,0:T(8,128)(2,1)}, u32[]{:S(2)}) copy-start(bf16[80,5120]{1,0:T(8,128)(2,1)} %get-tuple-element.94) | copy-start | bytes 2457604
